TPU v7x, 32 devices: a whole 2x2x4 slice. The times are simulated.
32 devices in a mesh: genes: 32 (over z, y, x, core).
Axes of the slice: x: 2, y: 2, z: 4, core: 2. Of those that a mesh axis runs over, the one named last changes fastest.
Arguments:
- expression: bfloat16 [32768, 1024], P('genes'), may hold values from -10 to 20
- labels: int32 [32768], P('genes'), may hold values from 0 to 399
Outputs:
- membership: float32 [32768, 400], P('genes')
- eigengenes: bfloat16 [400, 1024], replicated
All inputs are finite; a program needn't handle non-finite values.
Results may differ from a plain program's by a relative error of at most 0.0012.
The roundings to bfloat16 on the way count: a program that leaves them out, or rounds other values in their place, can miss the bound.
Values may be sent and summed in bfloat16 or wider, within the bound.
No kernel may reach another device: no remote copies, remote signals or barrier semaphores. Data moves between devices by JAX's collectives and lax.ppermute only.
A program may use at most 64 MiB of HBM per device.

v0:
```python
import jax
import jax.numpy as jnp
from jax import lax
from jax.sharding import PartitionSpec as P

SAMPLES = 1024
MODULES = 400
ITERS = 2
epsilon = 1e-05
sharpness = 30.0


def standardize(expression):
    values = expression.astype(jnp.float32)
    centre = jnp.mean(values, axis=1, keepdims=True)
    shifted = values - centre
    spread = jnp.mean(shifted * shifted, axis=1, keepdims=True)
    return (shifted * lax.rsqrt(spread + epsilon)).astype(jnp.bfloat16)


def shards(expression, labels):
    standard = standardize(expression)
    module_ids = jnp.arange(MODULES, dtype=jnp.int32)
    weights = (labels[:, None] == module_ids[None, :]).astype(jnp.bfloat16)
    shares = None
    eigengenes = None
    for iteration in range(ITERS):
        partial_value = lax.dot_general(
            weights, standard, (((0,), (0,)), ((), ())), preferred_element_type=jnp.float32
        )
        module_sums = lax.psum(partial_value, "genes")
        scale = lax.rsqrt(jnp.mean(module_sums * module_sums, axis=1, keepdims=True) + epsilon)
        eigengenes = (module_sums * scale).astype(jnp.bfloat16)
        correlation = (
            lax.dot_general(
                standard, eigengenes, (((1,), (1,)), ((), ())), preferred_element_type=jnp.float32
            )
            / SAMPLES
        )
        raised = jnp.exp(sharpness * correlation)
        shares = raised / jnp.sum(raised, axis=1, keepdims=True)
        weights = shares.astype(jnp.bfloat16)
    return (MODULES * shares, eigengenes)


def solution(mesh):
    placed = (P("genes", None), P("genes"))
    return jax.shard_map(
        shards, mesh=mesh, in_specs=placed, out_specs=(P("genes", None), P()), check_vma=False
    )
```

profile of v0, /device:TPU:0, one launch (start us, length us, event | category | flops | bytes accessed | tf_op | source)
XLA Modules:
  0.0 299.7 jit_solution(1048506449199865023)
XLA Ops:
  7.2 0.0 copy-start
  7.2 0.0 all-reduce.3.cloned.1.call-start
  7.2 2.1 convert_reduce_fusion
  9.3 0.1 copy-done
  9.4 0.7 fusion.2
  10.1 0.0 copy-start.5
  10.1 0.5 fusion.3
  10.7 0.0 copy-start.2
  10.7 1.3 copy-done.2
  12.0 0.0 copy-done.5
  12.0 2.4 fusion.4
  14.4 0.0 copy-start.3
  14.4 0.0 all-reduce.3.cloned.1.call-update
  14.4 0.0 all-reduce.5.cloned.1.call-start
  14.5 135.1 %all-reduce.3.cloned.1.call-done = f32[400,1024]{1,0:T(8,128)} async-done(((f32[400,1024]{1,0:T(8,128)}), f32[400,1024]{1,0:T(8,128)}) %all-reduce.3.cloned.1.call-update) | async-done | bytes 1638416 | tf_op jit(solution)/shard_map/psum | solution.py:31
  149.6 1.6 multiply_reduce_fusion.1
  151.2 0.0 copy-done.3
  151.2 2.5 fusion.9
  153.7 2.2 fusion.6
  155.9 0.0 all-reduce.5.cloned.1.call-update
  155.9 132.3 %all-reduce.5.cloned.1.call-done = f32[400,1024]{1,0:T(8,128)} async-done(((f32[400,1024]{1,0:T(8,128)}), f32[400,1024]{1,0:T(8,128)}) %all-reduce.5.cloned.1.call-update) | async-done | bytes 1638416 | tf_op jit(solution)/shard_map/psum | solution.py:31
  288.3 0.0 copy-start.1
  288.3 1.7 multiply_reduce_fusion
  290.0 0.2 copy-done.1
  290.2 0.1 multiply_convert_fusion
  290.4 0.0 copy-start.4
  290.4 1.1 fusion.10
  291.5 0.0 copy-done.4
  291.5 1.4 divide_multiply_fusion
  (4 shorter events, 0.0 us)
Async XLA Ops:
  7.2 2.2 copy-start
  7.2 142.4 %all-reduce.3.cloned.1.call-start = ((), (), s32[]{:S(2)}) async-start(), calls=%async_computation | async-start | bytes 3276800 | tf_op jit(solution)/shard_map/psum | solution.py:31
  10.1 1.9 copy-start.5
  10.7 1.4 copy-start.2
  14.4 136.8 %copy-start.3 = (bf16[1024,1024]{1,0:T(8,128)(2,1)S(1)}, bf16[1024,1024]{1,0:T(8,128)(2,1)}, u32[]{:S(2)}) copy-start(bf16[1024,1024]{1,0:T(8,128)(2,1)} %copy-done.2) | copy-start | bytes 6291460
  14.4 273.8 %all-reduce.5.cloned.1.call-start = ((), (), s32[]{:S(2)}) async-start(), calls=%async_computation.1 | async-start | bytes 3276800 | tf_op jit(solution)/shard_map/psum | solution.py:31
  288.3 1.9 copy-start.1
  290.4 1.1 copy-start.4
Sparse Core Ops, SparseCore 0:
  14.6 134.9 all-reduce.2
  156.1 132.1 all-reduce.4
where the time goes:
time: 300 us
  waiting for transfers between devices  267 us (89%)
  between operations  14.1 us (5%)
  other arithmetic  8.28 us (3%)
  matrix products  8.17 us (3%)
    psum x2, waiting for transfers between devices, shards(): module_sums = lax.psum(partial_value, 'genes')  267 us
  transfers between devices with their start and end apart: 2, of which 2 were waited for; matrix products, arithmetic and copies ran while one was open for 0% of the time, Pallas kernels for 0%

commit v1 on v0

--- a/solution.py
+++ b/solution.py
@@ -28,7 +28,8 @@
         partial_value = lax.dot_general(
             weights, standard, (((0,), (0,)), ((), ())), preferred_element_type=jnp.float32
         )
-        module_sums = lax.psum(partial_value, "genes")
+        blocks = lax.all_gather(partial_value, "genes")
+        module_sums = jnp.sum(blocks, axis=0)
         scale = lax.rsqrt(jnp.mean(module_sums * module_sums, axis=1, keepdims=True) + epsilon)
         eigengenes = (module_sums * scale).astype(jnp.bfloat16)
         correlation = (

time: 300 us -> 635 us (2.12)
  waiting for transfers between devices: 267 us -> 571 us
  other arithmetic: 8.28 us -> 38.6 us
    all_gather x0 -> x2, waiting for transfers between devices: none -> 571 us  [shards(): blocks = lax.all_gather(partial_value, 'genes')]
    psum x2 -> x0, waiting for transfers between devices: 267 us -> none  [shards(): module_sums = lax.psum(partial_value, 'genes')]
    reduce_sum x0 -> x2, other arithmetic: none -> 33.3 us  [shards(): module_sums = jnp.sum(blocks, axis=0)]
where the time goes in v1:
time: 635 us
  waiting for transfers between devices  571 us (90%)
  other arithmetic  38.6 us (6%)
  between operations  14.1 us (2%)
  matrix products  8.54 us (1%)
    all_gather x2, waiting for transfers between devices, shards(): blocks = lax.all_gather(partial_value, 'genes')  571 us
    reduce_sum x2, other arithmetic, shards(): module_sums = jnp.sum(blocks, axis=0)  33.3 us
  transfers between devices with their start and end apart: 2, of which 2 were waited for; matrix products, arithmetic and copies ran while one was open for 0% of the time, Pallas kernels for 0%

profile of v1, /device:TPU:0, one launch (start us, length us, event | category | flops | bytes accessed | tf_op | source)
XLA Modules:
  0.0 635.0 jit_solution(12211244244536334628)
XLA Ops:
  7.2 0.0 copy-start
  7.2 0.0 all-gather.5.cloned.1.call-start
  7.2 2.1 convert_reduce_fusion
  9.3 0.1 copy-done
  9.4 0.7 fusion.2
  10.1 0.0 copy-start.5
  10.1 0.5 fusion.3
  10.7 0.0 copy-start.1
  10.7 1.4 copy-done.1
  12.0 0.0 copy-done.5
  12.0 2.4 fusion.4
  14.4 0.0 all-gather.5.cloned.1.call-update
  14.4 0.0 all-gather.7.cloned.1.call-start
  14.5 287.6 %all-gather.5.cloned.1.call-done = f32[12800,1024]{1,0:T(8,128)} async-done(((f32[400,1024]{1,0:T(8,128)}), f32[12800,1024]{1,0:T(8,128)}) %all-gather.5.cloned.1.call-update) | async-done | bytes 52428816 | tf_op jit(solution)/shard_map/all_gather | solution.py:31
  302.1 16.7 %reduce_sum.74 = f32[400,1024]{1,0:T(8,128)S(1)} reduce(f32[32,400,1024]{2,1,0:T(8,128)} %bitcast.7, f32[]{:T(128)} %constant.16.clone.1), dimensions={0}, to_apply=%region_2.0 | reduce | flops 12697600 | bytes 54067204 | tf_op jit(solution)/shard_map/reduce_sum | solution.py:32
  318.8 0.2 multiply_reduce_fusion.1
  319.0 0.0 copy-start.2
  319.0 2.8 fusion.9
  321.8 0.0 copy-done.2
  321.8 2.2 fusion.6
  324.0 0.0 all-gather.7.cloned.1.call-update
  324.1 283.1 %all-gather.7.cloned.1.call-done = f32[12800,1024]{1,0:T(8,128)} async-done(((f32[400,1024]{1,0:T(8,128)}), f32[12800,1024]{1,0:T(8,128)}) %all-gather.7.cloned.1.call-update) | async-done | bytes 52428816 | tf_op jit(solution)/shard_map/all_gather | solution.py:31
  607.2 16.7 %reduce_sum.77 = f32[400,1024]{1,0:T(8,128)S(1)} reduce(f32[32,400,1024]{2,1,0:T(8,128)} %bitcast.8, f32[]{:T(128)} %constant.16.clone.1), dimensions={0}, to_apply=%region_5.0 | reduce | flops 12697600 | bytes 54067204 | tf_op jit(solution)/shard_map/reduce_sum | solution.py:32
  623.8 0.2 multiply_reduce_fusion
  624.0 0.0 copy-start.3
  624.0 0.2 multiply_convert_fusion
  624.2 1.4 copy-done.3
  625.6 0.0 copy-start.4
  625.6 1.1 fusion.10
  626.7 0.0 copy-done.4
  626.7 1.4 divide_multiply_fusion
  (4 shorter events, 0.0 us)
Async XLA Ops:
  7.2 2.2 copy-start
  7.2 294.9 %all-gather.5.cloned.1.call-start = ((), (), s32[]{:S(2)}) async-start(), calls=%async_computation | async-start | bytes 54067200 | tf_op jit(solution)/shard_map/all_gather | solution.py:31
  10.1 1.9 copy-start.5
  10.7 1.4 copy-start.1
  14.4 592.7 %all-gather.7.cloned.1.call-start = ((), (), s32[]{:S(2)}) async-start(), calls=%async_computation.1 | async-start | bytes 54067200 | tf_op jit(solution)/shard_map/all_gather | solution.py:31
  319.0 2.8 copy-start.2
  624.0 1.6 copy-start.3
  625.6 1.1 copy-start.4
Sparse Core Ops, SparseCore 0:
  14.6 287.4 all-gather.4
  324.2 282.9 all-gather.6
